TPU v7x, 32 devices: a whole 2x2x4 slice. The times are simulated.
32 devices in a mesh: member: 4 (over y, core), space: 8 (over z, x).
Axes of the slice: x: 2, y: 2, z: 4, core: 2. Of those that a mesh axis runs over, the one named last changes fastest.
Arguments:
- state: float32 [256, 128, 1024], P('member', 'space'), may hold values from -8 to 8
- obs_index: int32 [8192], P('space'), may hold values from 0 to 16383
- obs_value: float32 [8192], P('space'), may hold values from -6 to 6
- obs_scale: float32 [8192], P('space'), may hold values from 0.3 to 3
- ksat: float32 [128, 1024], P('space'), may hold values from 0.05 to 0.2
- storage: float32 [128, 1024], P('space'), may hold values from 0.5 to 4
- recharge: float32 [128, 1024], P('space'), may hold values from -1.8 to 1.8
- newton_counts: int32 [256], replicated, may hold values from 1 to 8, as said below
Outputs:
- forecast: float32 [256, 128, 1024], P('member', 'space')
Inputs may be any that keep to these rules, and one draw needn't show every extreme that they name: `newton_counts`: A count of 8 occurs in every draw.
All inputs are finite; a program needn't handle non-finite values.
Results may differ from a plain program's by a relative error of at most 0.0003.
Values sent between devices are 32-bit elements; how exact they have to be, the bound alone decides.
A program may use at most 64 MiB of HBM per device.

v0:
```python
import jax
import jax.numpy as jnp
from jax import lax
from jax.sharding import PartitionSpec as P

KMAX = 8
NS_ITERS = 12


HIGHEST_PRECISION = lax.Precision.HIGHEST
DAMPING = 0.3


def padded_2(array, sides, width):
    for axis, dim in sides:
        peers, length = (lax.axis_size(axis), array.shape[dim])
        up = [(i, (i + 1) % peers) for i in range(peers - 1)]
        down = [(j, i) for i, j in up]
        last = lax.slice_in_dim(array, length - width, length, axis=dim)
        leading = lax.slice_in_dim(array, 0, width, axis=dim)
        before = lax.ppermute(last, axis, up)
        after = lax.ppermute(leading, axis, down)
        array = jnp.concatenate([before, array, after], axis=dim)
    return array


def inverse_root(gram_matrix):
    order_size = gram_matrix.shape[0]
    identity = jnp.eye(order_size, dtype=jnp.float32)
    whole = identity + gram_matrix
    norm_value = jnp.sqrt(jnp.sum(whole * whole))
    upper_iter = whole / norm_value
    lower_iter = identity
    for sweep_index in range(NS_ITERS):
        middle = 1.5 * identity - 0.5 * jnp.dot(lower_iter, upper_iter, precision=HIGHEST_PRECISION)
        upper_iter = jnp.dot(upper_iter, middle, precision=HIGHEST_PRECISION)
        lower_iter = jnp.dot(middle, lower_iter, precision=HIGHEST_PRECISION)
    return lower_iter / jnp.sqrt(norm_value)


def face_flux(padded, conduct):
    wide_level = jnp.pad(padded, ((0, 0), (0, 0), (1, 1)))
    wide_cond = jnp.pad(conduct, ((0, 0), (0, 0), (1, 1)))
    centre_level = wide_level[:, 1:-1, 1:-1]
    centre_cond = wide_cond[:, 1:-1, 1:-1]
    height = centre_level.shape[1]
    breadth = centre_level.shape[2]
    divergence = jnp.zeros_like(centre_level)
    for offset_row, offset_col in ((0, 1), (2, 1), (1, 0), (1, 2)):
        other_level = wide_level[
            :, offset_row : offset_row + height, offset_col : offset_col + breadth
        ]
        other_cond = wide_cond[
            :, offset_row : offset_row + height, offset_col : offset_col + breadth
        ]
        divergence = divergence + 0.5 * (centre_cond + other_cond) * (other_level - centre_level)
    return divergence


def sweep_group(start_iter, goal, storage, group_counts):

    def sweep_once(sweep_index, iterate):
        bend_value = jnp.tanh(iterate)
        derivative = 1.0 + storage * (1.0 - bend_value * bend_value)
        stepped = iterate - DAMPING * (iterate + storage * bend_value - goal) / derivative
        return jnp.where((group_counts > sweep_index)[:, None, None], stepped, iterate)

    return lax.fori_loop(0, jnp.max(group_counts), sweep_once, start_iter)


def relax(pressure, drive_term, storage, counts):
    target = pressure + storage * jnp.tanh(pressure) + drive_term
    pieces = []
    for first_member in range(0, pressure.shape[0], 8):
        pieces.append(
            sweep_group(
                pressure[first_member : first_member + 8],
                target[first_member : first_member + 8],
                storage,
                counts[first_member : first_member + 8],
            )
        )
    return jnp.concatenate(pieces, axis=0)


def advance(padded, padded_ksat, storage, recharge, counts):
    conduct = padded_ksat * jax.nn.sigmoid(padded)
    drive_term = face_flux(padded, conduct) + recharge
    return relax(padded[:, 1:-1], drive_term, storage, counts)


def on_device(state, obs_index, obs_value, obs_scale, ksat, storage, recharge, newton_counts):
    local_members, tile_rows, tile_width = state.shape
    groups = lax.axis_size("member")
    members = local_members * groups
    tile_cells = tile_rows * tile_width
    block_cells = tile_cells // groups
    share = local_members // groups
    position = lax.axis_index("member")
    regrouped = lax.all_to_all(
        state.reshape(local_members, tile_cells), "member", split_axis=1, concat_axis=0, tiled=True
    )
    mean_state = jnp.mean(regrouped, axis=0)
    anomaly = regrouped - mean_state
    local_cell = obs_index - position * block_cells
    inside = (local_cell >= 0) & (local_cell < block_cells)
    picked = jnp.clip(local_cell, 0, block_cells - 1)
    weight = jnp.where(inside, obs_scale, 0.0)
    root_count = jnp.sqrt(jnp.float32(members - 1))
    spread = jnp.take(anomaly, picked, axis=1) * weight / root_count
    innovation = weight * (obs_value - jnp.take(mean_state, picked))
    gram_part = jnp.dot(spread, spread.T, precision=HIGHEST_PRECISION)
    drive_part = jnp.dot(spread, innovation, precision=HIGHEST_PRECISION)
    gram_matrix, drive_vector = lax.psum((gram_part, drive_part), ("member", "space"))
    root_inverse = inverse_root(gram_matrix)
    mean_weights = jnp.dot(
        root_inverse,
        jnp.dot(root_inverse, drive_vector, precision=HIGHEST_PRECISION),
        precision=HIGHEST_PRECISION,
    )
    transform = mean_weights[:, None] / root_count + root_inverse
    sequence = jnp.arange(members, dtype=jnp.int32)
    owner_of = sequence // local_members
    sort_key = owner_of * ((KMAX + 1) * members) + (KMAX - newton_counts) * members + sequence
    ranking = jnp.argsort(sort_key)
    member_ids = ranking.reshape(groups, share, groups).transpose(2, 0, 1).reshape(members)
    transform = jnp.take(transform, member_ids, axis=1)
    own_ids = lax.dynamic_slice_in_dim(member_ids, position * local_members, local_members)
    own_counts = jnp.take(newton_counts, own_ids)
    analysis = mean_state + jnp.dot(transform.T, anomaly, precision=HIGHEST_PRECISION)
    owned = lax.all_to_all(analysis, "member", split_axis=0, concat_axis=1, tiled=True)
    pressure = owned.reshape(local_members, tile_rows, tile_width)
    stacked = jnp.concatenate([pressure, ksat[None]], axis=0)
    widened = padded_2(stacked, (("space", 1),), 1)
    ksat_wide = widened[local_members]
    pressure = advance(widened[:local_members], ksat_wide, storage, recharge, own_counts)
    widened = padded_2(pressure, (("space", 1),), 1)
    pressure = advance(widened, ksat_wide, storage, recharge, own_counts)
    final_field = pressure.reshape(local_members, tile_cells)
    arrived = lax.all_to_all(final_field, "member", split_axis=0, concat_axis=0, tiled=True)
    by_owner = member_ids.reshape(groups, groups, share)
    arrived_ids = (
        jnp.take(by_owner, position, axis=1).reshape(local_members) - position * local_members
    )
    final_field = jnp.take(arrived, jnp.argsort(arrived_ids), axis=0)
    return final_field.reshape(local_members, tile_rows, tile_width)


def solution(mesh):
    return jax.shard_map(
        on_device,
        mesh=mesh,
        in_specs=(
            P("member", "space", None),
            P("space"),
            P("space"),
            P("space"),
            P("space", None),
            P("space", None),
            P("space", None),
            P(),
        ),
        out_specs=P("member", "space", None),
        check_vma=False,
    )
```

profile of v0, /device:TPU:8, one launch (start us, length us, event | category | flops | bytes accessed | tf_op | source)
XLA Modules:
  0.0 656.5 jit_solution(13870586919959672134)
XLA Ops:
  6.5 5.8 all_to_all.34
  12.4 6.6 %copy.22 = f32[64,4,4096]{2,0,1:T(8,128)} copy(f32[64,4,4096]{2,1,0:T(4,128)} %all_to_all.34) | data formatting | bytes 8388608 | tf_op jit(solution)/shard_map/all_to_all | solution.py:100
  19.0 5.0 all-to-all-start
  27.6 44.5 %all-to-all-done = f32[64,4,4096]{2,0,1:T(8,128)} async-done(((f32[64,4,4096]{2,0,1:T(8,128)}), f32[64,4,4096]{2,0,1:T(8,128)}, u32[]{:S(2)}, u32[]{:S(2)}) %all-to-all-start) | async-done | bytes 4194336 | tf_op jit(solution)/shard_map/all_to_all | solution.py:100
  74.6 6.2 gather_fusion.1
  80.7 4.8 bitcast_subtract_fusion
  85.5 5.6 copy.24
  91.1 5.7 gather_fusion
  100.8 39.6 %psum.15 = f32[256]{0:T(256)S(1)} all-reduce(f32[256]{0:T(256)S(1)} %bitcast.112), channel_id=1, replica_groups=mesh['member'=4,'space'=8] {'member','space'}, use_global_device_ids=true, to_apply=%region_5.6 | all-reduce | flops 256 | bytes 2048 | tf_op jit(solution)/shard_map/psum | solution.py:114
  140.4 86.6 %all-reduce.6.cloned.1.call-done = f32[256,256]{1,0:T(8,128)} async-done(((f32[256,256]{1,0:T(8,128)}), f32[256,256]{1,0:T(8,128)}) %all-reduce.6.cloned.1.call-update) | async-done | bytes 262160 | tf_op jit(solution)/shard_map/psum | solution.py:114
  247.0 8.2 %convolution_add_fusion = f32[256,4096]{1,0:T(8,128)} fusion(f32[256,4096]{1,0:T(8,128)} %bitcast_subtract_fusion, f32[4096]{0:T(1024)S(1)} %broadcast_multiply_fusion, f32[256,256]{1,0:T(8,128)S(1)} %gather_fusion.2, pred[256]{0:T(512)(128)(4,1)S(1)} %compare_and_fusion.1), kind=kOutput, calls=%fused_computation.51 | convolution fusion | flops 3222339584 | bytes 8667392 | tf_op jit(solution)/shard_map/dot_general | solution.py:130
  255.2 4.8 all-to-all-start.1
  262.5 45.8 %all-to-all-done.1 = f32[4,64,4096]{2,1,0:T(8,128)} async-done(((f32[4,64,4096]{2,1,0:T(8,128)}), f32[4,64,4096]{2,1,0:T(8,128)}, u32[]{:S(2)}, u32[]{:S(2)}) %all-to-all-start.1) | async-done | bytes 4194336 | tf_op jit(solution)/shard_map/all_to_all | solution.py:131
  308.3 6.9 %copy.28 = f32[64,4,4096]{2,1,0:T(4,128)} copy(f32[64,4,4096]{2,0,1:T(8,128)} %bitcast.13) | data formatting | bytes 8388608 | tf_op jit(solution)/shard_map/all_to_all | solution.py:131
  315.2 5.8 reshape.171
  321.0 3.6 pad_maximum_fusion.11
  324.6 3.4 collective-permute-start
  328.0 3.5 collective-permute-start.1
  331.5 3.3 fusion.69
  359.2 3.8 pad_maximum_fusion
  363.1 15.7 %fusion.6 = f32[64,16,1024]{2,1,0:T(8,128)} fusion(f32[64,18,1024]{2,1,0:T(8,128)S(1)} %get-tuple-element.768, f32[64,16,1024]{2,1,0:T(8,128)S(1)} %copy-done.2, f32[64,18,1024]{2,1,0:T(8,128)S(1)} %get-tuple-element.767, f32[65,1,1024]{2,1,0:T(1,128)} %collective-permute-done.1, f32[1,16,1024]{2,1,0:T(8,128)S(1)} %bitcast.106, ...), kind=kLoop, calls=%fused_computation.58 | loop fusion | flops 28311552 | bytes 34283520 | tf_op jit(solution)/shard_map/add | solution.py:72
  378.8 4.1 fusion.68
  382.9 6.3 while.168
  389.3 9.4 %while.167 = (s32[]{:T(128)}, f32[8,16,1024]{2,1,0:T(8,128)}, s32[]{:T(128)}, s32[8]{0:T(128)S(1)}, f32[16,1024]{1,0:T(8,128)S(1)}, /*index=5*/f32[8,16,1024]{2,1,0:T(8,128)}, s32[]{:T(128)}) while((s32[]{:T(128)}, f32[8,16,1024]{2,1,0:T(8,128)}, s32[]{:T(128)}, s32[8]{0:T(128)S(1)}, f32[16,1024]{1,0:T(8,128)S(1)}, ...), condition=%wide.region_26.27_spmd, body=%wide.region_25.26_spmd.sunk | while | flops 1441802 | bytes 1638537 | solution.py:68
  398.7 4.9 while.166
  403.6 6.9 %while.165 = (s32[]{:T(128)}, f32[8,16,1024]{2,1,0:T(8,128)S(1)}, s32[]{:T(128)}, s32[8]{0:T(128)S(1)}, f32[16,1024]{1,0:T(8,128)S(1)}, /*index=5*/f32[8,16,1024]{2,1,0:T(8,128)}, s32[]{:T(128)}) while((s32[]{:T(128)}, f32[8,16,1024]{2,1,0:T(8,128)S(1)}, s32[]{:T(128)}, s32[8]{0:T(128)S(1)}, f32[16,1024]{1,0:T(8,128)S(1)}, ...), condition=%wide.region_20.21_spmd, body=%wide.region_19.20_spmd.sunk | while | flops 1441802 | bytes 1638537 | solution.py:68
  410.5 7.2 %while.164 = (s32[]{:T(128)}, f32[8,16,1024]{2,1,0:T(8,128)S(1)}, s32[]{:T(128)}, s32[8]{0:T(128)S(1)}, f32[16,1024]{1,0:T(8,128)S(1)}, /*index=5*/f32[8,16,1024]{2,1,0:T(8,128)}, s32[]{:T(128)}) while((s32[]{:T(128)}, f32[8,16,1024]{2,1,0:T(8,128)S(1)}, s32[]{:T(128)}, s32[8]{0:T(128)S(1)}, f32[16,1024]{1,0:T(8,128)S(1)}, ...), condition=%wide.region_17.18_spmd, body=%wide.region_16.17_spmd.sunk | while | flops 1441802 | bytes 1638537 | solution.py:68
  417.7 16.9 %while.163 = (s32[]{:T(128)}, f32[8,16,1024]{2,1,0:T(8,128)S(1)}, s32[]{:T(128)}, s32[8]{0:T(128)S(1)}, f32[16,1024]{1,0:T(8,128)S(1)}, /*index=5*/f32[8,16,1024]{2,1,0:T(8,128)}, s32[]{:T(128)}) while((s32[]{:T(128)}, f32[8,16,1024]{2,1,0:T(8,128)S(1)}, s32[]{:T(128)}, s32[8]{0:T(128)S(1)}, f32[16,1024]{1,0:T(8,128)S(1)}, ...), condition=%wide.region_14.15_spmd, body=%wide.region_13.14_spmd.sunk | while | flops 1441802 | bytes 1638537 | solution.py:68
  434.6 4.6 while.162
  439.1 17.4 %while.161 = (s32[]{:T(128)}, f32[8,16,1024]{2,1,0:T(8,128)S(1)}, s32[]{:T(128)}, s32[8]{0:T(128)S(1)}, f32[16,1024]{1,0:T(8,128)S(1)}, /*index=5*/f32[8,16,1024]{2,1,0:T(8,128)}, s32[]{:T(128)}) while((s32[]{:T(128)}, f32[8,16,1024]{2,1,0:T(8,128)S(1)}, s32[]{:T(128)}, s32[8]{0:T(128)S(1)}, f32[16,1024]{1,0:T(8,128)S(1)}, ...), condition=%wide.region_8.9_spmd, body=%wide.region_7.8_spmd.sunk | while | flops 1441802 | bytes 1638537 | solution.py:68
  463.6 4.3 collective-permute-start.3
  467.9 6.3 collective-permute-done.2
  477.0 3.8 pad_maximum_fusion.3
  480.9 11.3 %fusion.18 = f32[64,16,1024]{2,1,0:T(8,128)} fusion(f32[64,18,1024]{2,1,0:T(8,128)S(1)} %get-tuple-element.770, f32[64,16,1024]{2,1,0:T(8,128)S(1)} %copy-done.8, f32[64,18,1024]{2,1,0:T(8,128)S(1)} %get-tuple-element.769, f32[64,1,1024]{2,1,0:T(1,128)} %collective-permute-done.3, f32[64,1,1024]{2,1,0:T(1,128)S(1)} %collective-permute-done.2, ...), kind=kLoop, calls=%fused_computation.70 | loop fusion | flops 26214400 | bytes 34209792 | tf_op jit(solution)/shard_map/add | solution.py:72
  492.2 4.1 fusion.66
  496.3 6.3 while.176
  502.7 9.4 %while.175 = (s32[]{:T(128)}, f32[8,16,1024]{2,1,0:T(8,128)}, s32[]{:T(128)}, s32[8]{0:T(128)S(1)}, f32[16,1024]{1,0:T(8,128)S(1)}, /*index=5*/f32[8,16,1024]{2,1,0:T(8,128)}, s32[]{:T(128)}) while((s32[]{:T(128)}, f32[8,16,1024]{2,1,0:T(8,128)}, s32[]{:T(128)}, s32[8]{0:T(128)S(1)}, f32[16,1024]{1,0:T(8,128)S(1)}, ...), condition=%wide.region_43.44_spmd, body=%wide.region_42.43_spmd.sunk | while | flops 1441802 | bytes 1638537 | solution.py:68
  512.0 4.9 while.174
  517.0 6.6 %while.173 = (s32[]{:T(128)}, f32[8,16,1024]{2,1,0:T(8,128)S(1)}, s32[]{:T(128)}, s32[8]{0:T(128)S(1)}, f32[16,1024]{1,0:T(8,128)S(1)}, /*index=5*/f32[8,16,1024]{2,1,0:T(8,128)}, s32[]{:T(128)}) while((s32[]{:T(128)}, f32[8,16,1024]{2,1,0:T(8,128)S(1)}, s32[]{:T(128)}, s32[8]{0:T(128)S(1)}, f32[16,1024]{1,0:T(8,128)S(1)}, ...), condition=%wide.region_39.40_spmd, body=%wide.region_38.39_spmd.sunk | while | flops 1441802 | bytes 1638537 | solution.py:68
  523.6 7.2 %while.172 = (s32[]{:T(128)}, f32[8,16,1024]{2,1,0:T(8,128)S(1)}, s32[]{:T(128)}, s32[8]{0:T(128)S(1)}, f32[16,1024]{1,0:T(8,128)S(1)}, /*index=5*/f32[8,16,1024]{2,1,0:T(8,128)}, s32[]{:T(128)}) while((s32[]{:T(128)}, f32[8,16,1024]{2,1,0:T(8,128)S(1)}, s32[]{:T(128)}, s32[8]{0:T(128)S(1)}, f32[16,1024]{1,0:T(8,128)S(1)}, ...), condition=%wide.region_37.38_spmd, body=%wide.region_36.37_spmd.sunk | while | flops 1441802 | bytes 1638537 | solution.py:68
  530.8 16.9 %while.171 = (s32[]{:T(128)}, f32[8,16,1024]{2,1,0:T(8,128)S(1)}, s32[]{:T(128)}, s32[8]{0:T(128)S(1)}, f32[16,1024]{1,0:T(8,128)S(1)}, /*index=5*/f32[8,16,1024]{2,1,0:T(8,128)}, s32[]{:T(128)}) while((s32[]{:T(128)}, f32[8,16,1024]{2,1,0:T(8,128)S(1)}, s32[]{:T(128)}, s32[8]{0:T(128)S(1)}, f32[16,1024]{1,0:T(8,128)S(1)}, ...), condition=%wide.region_35.36_spmd, body=%wide.region_34.35_spmd.sunk | while | flops 1441802 | bytes 1638537 | solution.py:68
  547.7 4.6 while.170
  552.3 17.4 %while.169 = (s32[]{:T(128)}, f32[8,16,1024]{2,1,0:T(8,128)S(1)}, s32[]{:T(128)}, s32[8]{0:T(128)S(1)}, f32[16,1024]{1,0:T(8,128)S(1)}, /*index=5*/f32[8,16,1024]{2,1,0:T(8,128)}, s32[]{:T(128)}) while((s32[]{:T(128)}, f32[8,16,1024]{2,1,0:T(8,128)S(1)}, s32[]{:T(128)}, s32[8]{0:T(128)S(1)}, f32[16,1024]{1,0:T(8,128)S(1)}, ...), condition=%wide.region_31.32_spmd, body=%wide.region_30.31_spmd.sunk | while | flops 1441802 | bytes 1638537 | solution.py:68
  576.3 5.0 all_to_all.41
  581.3 5.1 all-to-all-start.2
  589.3 45.2 %all-to-all-done.2 = f32[4,16,16384]{2,1,0:T(8,128)} async-done(((f32[4,16,16384]{2,1,0:T(8,128)}), f32[4,16,16384]{2,1,0:T(8,128)}, u32[]{:S(2)}, u32[]{:S(2)}) %all-to-all-start.2) | async-done | bytes 4194336 | tf_op jit(solution)/shard_map/all_to_all | solution.py:140
  634.6 7.7 %gather_fusion.4 = f32[64,16384]{1,0:T(8,128)} fusion(f32[64,16384]{1,0:T(8,128)} %bitcast.16, s32[1024]{0:T(1024)S(1)} %pad_clamp_fusion), kind=kCustom, calls=%fused_computation.4 | custom fusion | bytes 8388864 | tf_op jit(solution)/shard_map/jit(_take)/gather | solution.py:145
  642.3 4.6 copy.36
  (279 shorter events, 174.9 us)
Async XLA Ops:
  19.0 5.0 copy-start.1
  19.0 8.6 %copy-start.14 = (s32[1024]{0:T(1024)S(1)}, s32[1024]{0:T(1024)}, u32[]{:S(2)}) copy-start(s32[1024]{0:T(1024)} %param.41) | copy-start | bytes 12292
  19.0 53.2 %all-to-all-start = ((f32[64,4,4096]{2,0,1:T(8,128)}), f32[64,4,4096]{2,0,1:T(8,128)}, u32[]{:S(2)}, u32[]{:S(2)}) async-start(f32[64,4,4096]{2,0,1:T(8,128)} %copy.22), calls=%async_computation | async-start | bytes 8388608 | tf_op jit(solution)/shard_map/all_to_all | solution.py:100
  23.9 203.0 %all-reduce.6.cloned.1.call-start = ((), (), s32[]{:S(2)}) async-start(), calls=%async_computation.3 | async-start | bytes 524288 | tf_op jit(solution)/shard_map/psum | solution.py:114
  27.3 44.8 %copy-start.13 = (s32[4,16,4]{2,1,0:T(8,128)}, s32[4,16,4]{2,1,0:T(8,128)S(1)}, u32[]{:S(2)}) copy-start(s32[4,16,4]{2,1,0:T(8,128)S(1)} %reshape.168) | copy-start | bytes 3076
  91.1 5.7 copy-start.15
  91.1 5.7 copy-start.16
  255.2 53.0 %all-to-all-start.1 = ((f32[4,64,4096]{2,1,0:T(8,128)}), f32[4,64,4096]{2,1,0:T(8,128)}, u32[]{:S(2)}, u32[]{:S(2)}) async-start(f32[4,64,4096]{2,1,0:T(8,128)} %bitcast.102), calls=%async_computation.1 | async-start | bytes 8388608 | tf_op jit(solution)/shard_map/all_to_all | solution.py:131
  315.2 5.8 copy-start.9
  324.6 32.5 %collective-permute-start = (f32[65,1,1024]{2,1,0:T(1,128)}, f32[65,1,1024]{2,1,0:T(1,128)S(1)}, u32[]{:S(2)}, u32[]{:S(2)}) collective-permute-start(f32[65,1,1024]{2,1,0:T(1,128)} %get-tuple-element.771), channel_id=1, source_target_pairs={{0,1},{1,2},{2,3},{3,4},{4,5},{5,6},{6,7},{8,9},{9,10},{10,11},{11... | collective-permute-start | bytes 798728 | tf_op jit(solution)/shard_map/ppermute | solution.py:21
  328.0 29.1 %collective-permute-start.1 = (f32[65,1,1024]{2,1,0:T(1,128)}, f32[65,1,1024]{2,1,0:T(1,128)}, u32[]{:S(2)}, u32[]{:S(2)}) collective-permute-start(f32[65,1,1024]{2,1,0:T(1,128)} %get-tuple-element.772), channel_id=1, source_target_pairs={{1,0},{2,1},{3,2},{4,3},{5,4},{6,5},{7,6},{9,8},{10,9},{11,10},{12... | collective-permute-start | bytes 798728 | tf_op jit(solution)/shard_map/ppermute | solution.py:22
  357.0 2.2 copy-start.2
  359.2 3.8 copy-start.10
  359.2 3.8 copy-start
  359.2 3.8 copy-start.11
  378.8 4.1 copy-start.21
  382.9 6.4 copy-start.20
  389.2 9.4 %copy-start.19 = (s32[8]{0:T(128)S(1)}, s32[8]{0:T(128)}, u32[]{:S(2)}) copy-start(s32[8]{0:T(128)} %get-tuple-element.1693) | copy-start | bytes 100
  398.6 5.0 copy-start.18
  403.6 6.9 %copy-start.17 = (s32[8]{0:T(128)S(1)}, s32[8]{0:T(128)}, u32[]{:S(2)}) copy-start(s32[8]{0:T(128)} %get-tuple-element.1651) | copy-start | bytes 100
  456.5 1.0 copy-start.3
  456.6 1.2 copy-start.5
  457.8 2.0 copy-start.7
  461.1 13.1 %collective-permute-start.2 = (f32[64,1,1024]{2,1,0:T(1,128)}, f32[64,1,1024]{2,1,0:T(1,128)S(1)}, u32[]{:S(2)}, u32[]{:S(2)}) collective-permute-start(f32[64,1,1024]{2,1,0:T(1,128)} %get-tuple-element.781), channel_id=1, source_target_pairs={{0,1},{1,2},{2,3},{3,4},{4,5},{5,6},{6,7},{8,9},{9,10},{10,11},{11... | collective-permute-start | bytes 786440 | tf_op jit(solution)/shard_map/ppermute | solution.py:21
  463.6 13.4 %collective-permute-start.3 = (f32[64,1,1024]{2,1,0:T(1,128)}, f32[64,1,1024]{2,1,0:T(1,128)}, u32[]{:S(2)}, u32[]{:S(2)}) collective-permute-start(f32[64,1,1024]{2,1,0:T(1,128)} %get-tuple-element.782), channel_id=1, source_target_pairs={{1,0},{2,1},{3,2},{4,3},{5,4},{6,5},{7,6},{9,8},{10,9},{11,10},{12... | collective-permute-start | bytes 786440 | tf_op jit(solution)/shard_map/ppermute | solution.py:22
  467.9 13.0 %copy-start.8 = (f32[64,16,1024]{2,1,0:T(8,128)S(1)}, f32[64,16,1024]{2,1,0:T(8,128)}, u32[]{:S(2)}) copy-start(f32[64,16,1024]{2,1,0:T(8,128)} %copy-done.7) | copy-start | bytes 12582916
  467.9 13.0 %copy-start.12 = (f32[16,1024]{1,0:T(8,128)S(1)}, f32[16,1024]{1,0:T(8,128)}, u32[]{:S(2)}) copy-start(f32[16,1024]{1,0:T(8,128)} %param.46) | copy-start | bytes 196612
  569.7 5.0 copy-start.4
  569.7 5.8 copy-start.6
  581.3 53.3 %all-to-all-start.2 = ((f32[4,16,16384]{2,1,0:T(8,128)}), f32[4,16,16384]{2,1,0:T(8,128)}, u32[]{:S(2)}, u32[]{:S(2)}) async-start(f32[4,16,16384]{2,1,0:T(8,128)} %all_to_all.41), calls=%async_computation.2 | async-start | bytes 8388608 | tf_op jit(solution)/shard_map/all_to_all | solution.py:140
Sparse Core Ops, SparseCore 0:
  100.1 126.7 all-reduce.5
where the time goes:
time: 669 us; the launch traced here: 656 us
  waiting for transfers between devices  231 us (35%)
  other arithmetic  155 us (23%)
  local copies, waits for them, and re-layouts  109 us (16%)
  loops' own time  49.4 us (7%)
  blocking collectives  39.6 us (6%)
  starting transfers between devices  28.5 us (4%)
  matrix products  28.2 us (4%)
  between operations  15.5 us (2%)
    select_n x62, other arithmetic, sweep_once(): jnp.where((group_counts > sweep_index)[:, None, None], stepped, iterate)  97 us
    psum x1, waiting for transfers between devices, on_device(): lax.psum((gram_part, drive_part), ('member', 'space'))  86.6 us
    another operation x16, loops' own time, sweep_group(): return lax.fori_loop(0, jnp.max(group_counts), sweep_once, start_iter)  49.4 us
    all_to_all x1, waiting for transfers between devices, on_device(): lax.all_to_all(analysis, 'member', split_axis=0, concat_axis=1, tiled=True)  45.8 us
    all_to_all x1, waiting for transfers between devices, on_device(): lax.all_to_all(final_field, 'member', split_axis=0, concat_axis=0, tiled=...  45.2 us
    all_to_all x1, waiting for transfers between devices, on_device(): lax.all_to_all(state.reshape(local_members, tile_cells), 'member', split_...  44.5 us
    psum x1, blocking collectives, on_device(): lax.psum((gram_part, drive_part), ('member', 'space'))  39.6 us
    add x2, other arithmetic, relax(): target = pressure + storage * jnp.tanh(pressure) + drive_term  27 us
  transfers between devices with their start and end apart: 8, of which 6 were waited for; matrix products, arithmetic and copies ran while one was open for 5% of the time, Pallas kernels for 0%

commit v1 on v0

v1 whole, which is shorter than its diff:
```python
import functools

import jax
import jax.numpy as jnp
from jax import lax
from jax.experimental import pallas as pl
from jax.experimental.pallas import tpu as pltpu
from jax.sharding import PartitionSpec as P


NS_ITERS = 12
HIGHEST_PRECISION = lax.Precision.HIGHEST
DAMPING = 0.3
GROUP = 8


def inverse_root(gram_matrix):
    order_size = gram_matrix.shape[0]
    identity = jnp.eye(order_size, dtype=jnp.float32)
    whole = identity + gram_matrix
    norm_value = jnp.sqrt(jnp.sum(whole * whole))
    upper_iter = whole / norm_value
    lower_iter = identity
    for _ in range(NS_ITERS):
        middle = 1.5 * identity - 0.5 * jnp.dot(lower_iter, upper_iter, precision=HIGHEST_PRECISION)
        upper_iter = jnp.dot(upper_iter, middle, precision=HIGHEST_PRECISION)
        lower_iter = jnp.dot(middle, lower_iter, precision=HIGHEST_PRECISION)
    return lower_iter / jnp.sqrt(norm_value)


def halves(value):
    high = value.astype(jnp.bfloat16)
    low = (value - high.astype(jnp.float32)).astype(jnp.bfloat16)
    return high, low


def analysis_kernel(rows, count, *refs):
    weight_high, weight_low = halves(refs[0][...])
    pieces = refs[1 : 1 + count]
    out_ref, first_ref, last_ref = refs[1 + count :]
    own = weight_high.shape[0]
    both = jnp.concatenate([weight_high, weight_low], axis=0)
    for row in range(0, rows, 2):
        columns = []
        for line in (row, row + 1):
            stacked = [piece[pl.ds(line, piece.shape[0] // rows, stride=rows), :] for piece in pieces]
            columns.append(jnp.concatenate(stacked, axis=0))
        high, low = halves(jnp.concatenate(columns, axis=1))
        wide = jnp.dot(both, high, preferred_element_type=jnp.float32)
        result = wide[:own] + wide[own:]
        result = result + jnp.dot(weight_high, low, preferred_element_type=jnp.float32)
        lanes = out_ref.shape[1]
        for index, line in enumerate((row, row + 1)):
            out_ref[pl.ds(line, own, stride=rows), :] = result[:, index * lanes : (index + 1) * lanes]
        if row == 0:
            first_ref[...] = result[:, :lanes]
        if row == rows - 2:
            last_ref[...] = result[:, lanes:]


def analyse(weights, pieces, rows, width):
    own = weights.shape[0]
    total = weights.shape[1]
    block = 128
    flat = [piece.reshape(piece.shape[0] * rows, width) for piece in pieces]
    out, first, last = pl.pallas_call(
        functools.partial(analysis_kernel, rows, len(flat)),
        grid=(width // block,),
        in_specs=[pl.BlockSpec((own, total), lambda i: (0, 0))]
        + [pl.BlockSpec((piece.shape[0], block), lambda i: (0, i)) for piece in flat],
        out_specs=[
            pl.BlockSpec((own * rows, block), lambda i: (0, i)),
            pl.BlockSpec((own, block), lambda i: (0, i)),
            pl.BlockSpec((own, block), lambda i: (0, i)),
        ],
        out_shape=[
            jax.ShapeDtypeStruct((own * rows, width), jnp.float32),
            jax.ShapeDtypeStruct((own, width), jnp.float32),
            jax.ShapeDtypeStruct((own, width), jnp.float32),
        ],
        name="analyse",
    )(weights, *flat)
    return out.reshape(own, rows, width), first, last


def sigmoid(value):
    return 0.5 + 0.5 * jnp.tanh(0.5 * value)


def step_kernel(edges, counts_ref, field, above, below, ksat, ksat_above, ksat_below, storage, recharge, out, *sides):
    rows, width = ksat.shape
    base = pl.program_id(0) * field.shape[0]
    line = lax.broadcasted_iota(jnp.int32, (rows, width), 0)
    column = lax.broadcasted_iota(jnp.int32, (rows, width), 1)

    def shifted(value, before, after):
        up = jnp.where(line == 0, before, pltpu.roll(value, 1, axis=0))
        down = jnp.where(line == rows - 1, after, pltpu.roll(value, rows - 1, axis=0))
        left = jnp.where(column == 0, 0.0, pltpu.roll(value, 1, axis=1))
        right = jnp.where(column == width - 1, 0.0, pltpu.roll(value, width - 1, axis=1))
        return up, down, left, right

    def one_member(member, carry):
        level = field[member]
        level_above = above[pl.ds(member, 1), :]
        level_below = below[pl.ds(member, 1), :]
        conduct = ksat[...] * sigmoid(level)
        conduct_above = ksat_above[...] * sigmoid(level_above)
        conduct_below = ksat_below[...] * sigmoid(level_below)
        flux = jnp.zeros_like(level)
        others = shifted(level, level_above, level_below)
        other_conducts = shifted(conduct, conduct_above, conduct_below)
        for other, other_conduct in zip(others, other_conducts):
            flux = flux + (conduct + other_conduct) * (other - level)
        goal = level + storage[...] * jnp.tanh(level) + (0.5 * flux + recharge[...])

        def sweep(index, iterate):
            held = storage[...]
            bend = jnp.tanh(iterate)
            slope = 1.0 + held * (1.0 - bend * bend)
            guess = pl.reciprocal(slope, approx=True)
            inverse = guess * (2.0 - slope * guess)
            return iterate - DAMPING * (iterate + held * bend - goal) * inverse

        result = lax.fori_loop(0, counts_ref[base + member], sweep, level)
        out[member] = result
        if edges:
            sides[0][pl.ds(member, 1), :] = result[:1]
            sides[1][pl.ds(member, 1), :] = result[rows - 1 :]
        return carry

    lax.fori_loop(0, field.shape[0], one_member, 0)


def forecast_step(field, above, below, ksat, ksat_above, ksat_below, storage, recharge, counts, edges):
    own, rows, width = field.shape
    cell_spec = pl.BlockSpec((rows, width), lambda i, c: (0, 0))
    line_spec = pl.BlockSpec((1, width), lambda i, c: (0, 0))
    side_spec = pl.BlockSpec((GROUP, width), lambda i, c: (i, 0))
    field_spec = pl.BlockSpec((GROUP, rows, width), lambda i, c: (i, 0, 0))
    side_shape = jax.ShapeDtypeStruct((own, width), jnp.float32)
    return pl.pallas_call(
        functools.partial(step_kernel, edges),
        grid_spec=pltpu.PrefetchScalarGridSpec(
            num_scalar_prefetch=1,
            grid=(own // GROUP,),
            in_specs=[field_spec, side_spec, side_spec, cell_spec, line_spec, line_spec, cell_spec, cell_spec],
            out_specs=[field_spec] + [side_spec] * (2 * edges),
        ),
        out_shape=[jax.ShapeDtypeStruct(field.shape, jnp.float32)] + [side_shape] * (2 * edges),
        name="forecast_step",
    )(counts, field, above, below, ksat, ksat_above, ksat_below, storage, recharge)


def from_neighbours(first, last):
    peers = lax.axis_size("space")
    upward = [(i, i + 1) for i in range(peers - 1)]
    downward = [(i + 1, i) for i in range(peers - 1)]
    return lax.ppermute(last, "space", upward), lax.ppermute(first, "space", downward)


def on_device(state, obs_index, obs_value, obs_scale, ksat, storage, recharge, newton_counts):
    local, rows, width = state.shape
    groups = lax.axis_size("member")
    devices = groups * lax.axis_size("space")
    members = local * groups
    position = lax.axis_index("member")
    root_count = jnp.sqrt(jnp.float32(members - 1))
    swap = [(i, i ^ 1) for i in range(groups)]

    pieces = [(state, position, 0), (lax.ppermute(state, "member", swap), position ^ 1, 0)]

    def send_chunk(source, low, high):
        for distance in range(2, groups, 2):
            route = [(i, (i + distance) % groups) for i in range(groups)]
            arrived = lax.ppermute(source[low:high], "member", route)
            pieces.append((arrived, (position + groups - distance) % groups, low))
            pieces.append((lax.ppermute(arrived, "member", swap), ((position ^ 1) + groups - distance) % groups, low))

    early = 8
    send_chunk(state, 0, early)

    local_obs = jnp.take(state.reshape(local, rows * width), obs_index, axis=1)
    sampled = lax.all_to_all(local_obs, "member", split_axis=1, concat_axis=0, tiled=True)
    part = obs_index.shape[0] // groups
    scale = lax.dynamic_slice_in_dim(obs_scale, position * part, part)
    value = lax.dynamic_slice_in_dim(obs_value, position * part, part)
    mean_obs = jnp.mean(sampled, axis=0)
    spread = (sampled - mean_obs) * scale / root_count
    innovation = scale * (value - mean_obs)
    right = jnp.concatenate([spread, innovation[None], jnp.zeros((127, part), jnp.float32)], axis=0)
    partial = jnp.dot(spread, right.T, precision=HIGHEST_PRECISION)
    partial = partial.reshape(devices, members // devices, members + 128)
    partial = lax.all_to_all(partial, ("member", "space"), split_axis=0, concat_axis=0)
    summed = lax.all_gather(jnp.sum(partial, axis=0), ("member", "space"), axis=0, tiled=True)
    late_state, summed = lax.optimization_barrier((state, summed))

    middle = (early + local) // 2 // 8 * 8
    send_chunk(late_state, early, middle)
    send_chunk(late_state, middle, local)

    drive_vector = summed[:, members]
    root_inverse = inverse_root(summed[:, :members])
    mean_weights = jnp.dot(
        root_inverse,
        jnp.dot(root_inverse, drive_vector, precision=HIGHEST_PRECISION),
        precision=HIGHEST_PRECISION,
    )
    transform = mean_weights[:, None] / root_count + root_inverse
    own_columns = lax.dynamic_slice_in_dim(transform, position * local, local, axis=1)
    weights = (own_columns - jnp.mean(own_columns, axis=0) + 1.0 / members).T
    ordered = jnp.concatenate(
        [
            lax.dynamic_slice_in_dim(weights, source * local + low, piece.shape[0], axis=1)
            for piece, source, low in pieces
        ],
        axis=1,
    )
    field, first, last = analyse(ordered, [piece for piece, source, low in pieces], rows, width)

    counts = lax.dynamic_slice_in_dim(newton_counts, position * local, local)
    ksat_above, ksat_below = from_neighbours(ksat[:1], ksat[rows - 1 :])
    above, below = from_neighbours(first, last)
    field, first, last = forecast_step(
        field, above, below, ksat, ksat_above, ksat_below, storage, recharge, counts, True
    )
    above, below = from_neighbours(first, last)
    (field,) = forecast_step(
        field, above, below, ksat, ksat_above, ksat_below, storage, recharge, counts, False
    )
    return field


def solution(mesh):
    return jax.shard_map(
        on_device,
        mesh=mesh,
        in_specs=(
            P("member", "space", None),
            P("space"),
            P("space"),
            P("space"),
            P("space", None),
            P("space", None),
            P("space", None),
            P(),
        ),
        out_specs=P("member", "space", None),
        check_vma=False,
    )
```

time: 669 us -> 306 us (0.46)
  the two profiles are of different devices: /device:TPU:8 before, /device:TPU:25 now
where the time goes in v1:
time: 306 us; the launch traced here: 305 us
  waiting for transfers between devices  109 us (36%)
  blocking collectives  62.7 us (20%)
  Pallas kernels  61.9 us (20%)
  starting transfers between devices  31.3 us (10%)
  local copies, waits for them, and re-layouts  20.1 us (7%)
  matrix products  15.5 us (5%)
  other arithmetic  3.92 us (1%)
    ppermute x3, waiting for transfers between devices, send_chunk(): arrived = lax.ppermute(source[low:high], 'member', route)  89.4 us
    all_gather x1, blocking collectives, on_device(): lax.all_gather(jnp.sum(partial, axis=0), ('member', 'space'), axis=0, til...  62.7 us
    pallas_call x2, Pallas kernels, forecast_step(): pl.pallas_call(functools.partial(step_kernel, edges), grid_spec=pltpu.Pre...  48 us
    pallas_call x1, Pallas kernels, analyse(): pl.pallas_call(functools.partial(analysis_kernel, rows, len(flat)), grid=...  13.9 us
    ppermute x3, starting transfers between devices, from_neighbours(): lax.ppermute(first, 'space', downward)  10.4 us
    ppermute x3, waiting for transfers between devices, from_neighbours(): lax.ppermute(first, 'space', downward)  9.9 us
    unnamed x21, local copies, waits for them, and re-layouts  8.49 us
    ppermute x3, starting transfers between devices, from_neighbours(): lax.ppermute(last, 'space', upward)  7.19 us
  transfers between devices with their start and end apart: 15, of which 8 were waited for; matrix products, arithmetic and copies ran while one was open for 7% of the time, Pallas kernels for 0%

profile of v1, /device:TPU:25, one launch (start us, length us, event | category | flops | bytes accessed | tf_op | source)
XLA Modules:
  0.0 305.1 jit_solution(13805888219363277728)
XLA Ops:
  0.0 0.7 fusion.19
  0.7 0.7 compare_and_fusion
  1.4 7.0 %copy.11 = f32[64,16,1024]{0,2,1:T(8,128)} copy(f32[64,16,1024]{2,1,0:T(8,128)} %param.8) | data formatting | bytes 8388608 | tf_op args[0]
  8.3 6.2 %gather_fusion = f32[1024,64]{1,0:T(8,128)S(1)} fusion(f32[64,16384]{0,1:T(8,128)} %bitcast.119, s32[1024]{0:T(1024)S(1)} %fusion.19), kind=kCustom, calls=%fused_computation | custom fusion | bytes 528384 | tf_op jit(solution)/shard_map/jit(_take)/gather | solution.py:183
  14.7 0.7 broadcast_select_fusion
  15.5 4.0 %all-to-all-start = ((f32[64,4,256]{2,0,1:T(8,128)}), f32[64,4,256]{2,0,1:T(8,128)S(1)}, u32[]{:S(2)}, u32[]{:S(2)}) async-start(f32[64,4,256]{2,0,1:T(8,128)} %broadcast_select_fusion), calls=%async_computation | async-start | bytes 524288 | tf_op jit(solution)/shard_map/all_to_all | solution.py:184
  19.6 5.0 %all-to-all-done = f32[64,4,256]{2,0,1:T(8,128)S(1)} async-done(((f32[64,4,256]{2,0,1:T(8,128)}), f32[64,4,256]{2,0,1:T(8,128)S(1)}, u32[]{:S(2)}, u32[]{:S(2)}) %all-to-all-start) | async-done | bytes 262176 | tf_op jit(solution)/shard_map/all_to_all | solution.py:184
  24.6 0.8 subtract_multiply_fusion
  25.4 1.4 fusion
  26.8 5.5 %all-to-all-start.1 = ((f32[32,8,384]{2,1,0:T(8,128)}), f32[32,8,384]{2,1,0:T(8,128)S(1)}, u32[]{:S(2)}, u32[]{:S(2)}) async-start(f32[32,8,384]{2,1,0:T(8,128)} %fusion), calls=%async_computation.1 | async-start | bytes 786432 | tf_op jit(solution)/shard_map/all_to_all | solution.py:194
  32.3 1.1 slice.23
  33.4 1.3 collective-permute-start.1
  34.7 0.7 collective-permute-start
  35.4 15.1 %collective-permute-done.1 = f32[8,16,1024]{2,1,0:T(8,128)S(1)} collective-permute-done((f32[8,16,1024]{2,1,0:T(8,128)S(1)}, f32[8,16,1024]{2,1,0:T(8,128)S(1)}, u32[]{:S(2)}, u32[]{:S(2)}) %collective-permute-start.1) | collective-permute-done | bytes 524320 | tf_op jit(solution)/shard_map/ppermute | solution.py:176
  50.5 0.5 collective-permute-start.2
  51.1 62.7 %all_gather.3 = f32[256,384]{1,0:T(8,128)S(1)} all-gather(f32[8,384]{1,0:T(8,128)S(1)} %reduce_sum.37), channel_id=1, replica_groups=mesh['member'=4,'space'=8] {'member','space'}, dimensions={0}, use_global_device_ids=true | all-gather | bytes 405504 | tf_op jit(solution)/shard_map/all_gather | solution.py:195
  113.8 0.7 multiply_reduce_fusion
  115.5 0.4 fusion.15
  116.2 0.4 select_subtract_fusion.10
  117.4 0.4 select_subtract_fusion.9
  119.7 0.4 select_subtract_fusion.7
  124.6 1.3 slice.24
  125.9 0.7 collective-permute-start.5
  126.6 0.7 collective-permute-start.3
  128.5 0.4 select_subtract_fusion.2
  129.7 0.4 select_subtract_fusion.1
  130.1 0.6 fusion.42
  131.1 42.6 %collective-permute-done.5 = f32[32,16,1024]{2,1,0:T(8,128)S(1)} collective-permute-done((f32[32,16,1024]{2,1,0:T(8,128)S(1)}, f32[32,16,1024]{2,1,0:T(8,128)S(1)}, u32[]{:S(2)}, u32[]{:S(2)}) %collective-permute-start.5) | collective-permute-done | bytes 2097184 | tf_op jit(solution)/shard_map/ppermute | solution.py:176
  174.2 0.6 convolution_divide_fusion
  174.8 31.7 %collective-permute-done.3 = f32[24,16,1024]{2,1,0:T(8,128)} collective-permute-done((f32[24,16,1024]{2,1,0:T(8,128)}, f32[24,16,1024]{2,1,0:T(8,128)}, u32[]{:S(2)}, u32[]{:S(2)}) %collective-permute-start.3) | collective-permute-done | bytes 1572896 | tf_op jit(solution)/shard_map/ppermute | solution.py:176
  207.7 0.7 concatenate.7.refs_0_
  208.5 1.8 collective-permute-done.4
  210.3 13.9 %analyse.1 = (f32[1024,1024]{1,0:T(8,128)}, f32[64,1024]{1,0:T(8,128)}, f32[64,1024]{1,0:T(8,128)}) custom-call(f32[64,256]{1,0:T(8,128)} %concatenate.7.refs_0_, f32[1024,1024]{1,0:T(8,128)} %bitcast.118, f32[1024,1024]{1,0:T(8,128)} %bitcast.20.refs_2_, f32[128,1024]{1,0:T(8,128)} %bitcast.124, f32[128,1024]{1,0:T(8,128)} %bitcast.22.refs_4_, ...), custom_call_target="tpu_custom_call" | custom-call | tf_op jit(solution)/shard_map/analyse/pallas_call | solution.py:66
  224.2 1.9 collective-permute-start.7
  226.1 4.3 %collective-permute-start.8 = (f32[64,1024]{1,0:T(8,128)}, f32[64,1024]{1,0:T(8,128)S(1)}, u32[]{:S(2)}, u32[]{:S(2)}) collective-permute-start(f32[64,1024]{1,0:T(8,128)} %get-tuple-element.17), channel_id=1, source_target_pairs={{1,0},{2,1},{3,2},{4,3},{5,4},{6,5},{7,6},{9,8},{10,9},{11,10},{12... | collective-permute-start | bytes 786440 | tf_op jit(solution)/shard_map/ppermute | solution.py:159
  230.4 0.8 fusion.22
  231.2 1.9 collective-permute-start.10
  233.1 3.4 %collective-permute-start.9 = (f32[1,1024]{1,0:T(1,128)S(1)}, f32[1,1024]{1,0:T(1,128)S(1)}, u32[]{:S(2)}, u32[]{:S(2)}) collective-permute-start(f32[1,1024]{1,0:T(1,128)S(1)} %get-tuple-element.24), channel_id=1, source_target_pairs={{0,1},{1,2},{2,3},{3,4},{4,5},{5,6},{6,7},{8,9},{9,10},{10,11},{11... | collective-permute-start | bytes 12296 | tf_op jit(solution)/shard_map/ppermute | solution.py:159
  236.4 0.6 dynamic_slice.36.counts_ref
  237.0 4.2 %collective-permute-done.10.ksat_below = f32[1,1024]{1,0:T(1,128)S(1)} collective-permute-done((f32[1,1024]{1,0:T(1,128)S(1)}, f32[1,1024]{1,0:T(1,128)S(1)}, u32[]{:S(2)}, u32[]{:S(2)}) %collective-permute-start.10) | collective-permute-done | bytes 4128 | tf_op jit(solution)/shard_map/ppermute | solution.py:159
  241.3 0.6 copy-done.7
  242.1 24.2 %forecast_step.2 = (f32[64,16,1024]{2,1,0:T(8,128)}, f32[64,1024]{1,0:T(8,128)}, f32[64,1024]{1,0:T(8,128)}) custom-call(s32[64]{0:T(128)} %dynamic_slice.36.counts_ref, f32[64,16,1024]{2,1,0:T(8,128)} %bitcast.120, f32[64,1024]{1,0:T(8,128)} %copy-done.3, f32[64,1024]{1,0:T(8,128)} %copy-done.4, f32[16,1024]{1,0:T(8,128)} %ksat.3, f32[1,1024]{1,0:T(1,128)} %copy-done.8, ...), custom_call_target="tpu_custom_call" | custom-call | tf_op jit(solution)/shard_map/forecast_step/pallas_call | solution.py:142
  266.3 1.9 collective-permute-start.11
  268.2 4.3 %collective-permute-start.12 = (f32[64,1024]{1,0:T(8,128)}, f32[64,1024]{1,0:T(8,128)S(1)}, u32[]{:S(2)}, u32[]{:S(2)}) collective-permute-start(f32[64,1024]{1,0:T(8,128)} %get-tuple-element.20), channel_id=1, source_target_pairs={{1,0},{2,1},{3,2},{4,3},{5,4},{6,5},{7,6},{9,8},{10,9},{11,10},{12... | collective-permute-start | bytes 786440 | tf_op jit(solution)/shard_map/ppermute | solution.py:159
  272.4 2.4 collective-permute-done.11.above
  274.8 5.7 %collective-permute-done.12.below = f32[64,1024]{1,0:T(8,128)S(1)} collective-permute-done((f32[64,1024]{1,0:T(8,128)}, f32[64,1024]{1,0:T(8,128)S(1)}, u32[]{:S(2)}, u32[]{:S(2)}) %collective-permute-start.12) | collective-permute-done | bytes 262176 | tf_op jit(solution)/shard_map/ppermute | solution.py:159
  280.6 0.7 copy-done.6
  281.3 23.8 %forecast_step.3 = f32[64,16,1024]{2,1,0:T(8,128)} custom-call(s32[64]{0:T(128)} %dynamic_slice.36.counts_ref, f32[64,16,1024]{2,1,0:T(8,128)} %get-tuple-element.18.field, f32[64,1024]{1,0:T(8,128)} %copy-done.5, f32[64,1024]{1,0:T(8,128)} %copy-done.6, f32[16,1024]{1,0:T(8,128)} %ksat.3, f32[1,1024]{1,0:T(1,128)} %copy-done.8, f32[1,1024]{1,0:T(1,128)} %copy-done.7, ...), custom_call_target="tpu_custom_call" | custom-call | tf_op jit(solution)/shard_map/forecast_step/pallas_call | solution.py:142
  (73 shorter events, 12.3 us)
Async XLA Ops:
  15.5 9.1 %all-to-all-start = ((f32[64,4,256]{2,0,1:T(8,128)}), f32[64,4,256]{2,0,1:T(8,128)S(1)}, u32[]{:S(2)}, u32[]{:S(2)}) async-start(f32[64,4,256]{2,0,1:T(8,128)} %broadcast_select_fusion), calls=%async_computation | async-start | bytes 524288 | tf_op jit(solution)/shard_map/all_to_all | solution.py:184
  26.8 24.2 %all-to-all-start.1 = ((f32[32,8,384]{2,1,0:T(8,128)}), f32[32,8,384]{2,1,0:T(8,128)S(1)}, u32[]{:S(2)}, u32[]{:S(2)}) async-start(f32[32,8,384]{2,1,0:T(8,128)} %fusion), calls=%async_computation.1 | async-start | bytes 786432 | tf_op jit(solution)/shard_map/all_to_all | solution.py:194
  33.4 17.1 %collective-permute-start.1 = (f32[8,16,1024]{2,1,0:T(8,128)S(1)}, f32[8,16,1024]{2,1,0:T(8,128)S(1)}, u32[]{:S(2)}, u32[]{:S(2)}) collective-permute-start(f32[8,16,1024]{2,1,0:T(8,128)S(1)} %slice.23), channel_id=1, source_target_pairs={{0,16},{8,24},{16,0},{24,8},{1,17},{9,25},{17,1},{25,9},{2,18},{10... | collective-permute-start | bytes 1572872 | tf_op jit(solution)/shard_map/ppermute | solution.py:176
  34.7 175.6 %collective-permute-start = (f32[64,16,1024]{2,1,0:T(8,128)}, f32[64,16,1024]{2,1,0:T(8,128)}, u32[]{:S(2)}, u32[]{:S(2)}) collective-permute-start(f32[64,16,1024]{2,1,0:T(8,128)} %param.8), channel_id=1, source_target_pairs={{0,8},{8,0},{16,24},{24,16},{1,9},{9,1},{17,25},{25,17},{2,10},{10... | collective-permute-start | bytes 12582920 | tf_op jit(solution)/shard_map/ppermute | solution.py:171
  50.5 68.0 %copy-start.2 = (f32[8,16,1024]{2,1,0:T(8,128)}, f32[8,16,1024]{2,1,0:T(8,128)S(1)}, u32[]{:S(2)}) copy-start(f32[8,16,1024]{2,1,0:T(8,128)S(1)} %collective-permute-done.1) | copy-start | bytes 1572868
  50.5 158.0 %collective-permute-start.2 = (f32[8,16,1024]{2,1,0:T(8,128)S(1)}, f32[8,16,1024]{2,1,0:T(8,128)}, u32[]{:S(2)}, u32[]{:S(2)}) collective-permute-start(f32[8,16,1024]{2,1,0:T(8,128)S(1)} %collective-permute-done.1), channel_id=1, source_target_pairs={{0,8},{8,0},{16,24},{24,16},{1,9},{9,1},{17,25},{25,17},{2,10},{10... | collective-permute-start | bytes 1572872 | tf_op jit(solution)/shard_map/ppermute | solution.py:178
  120.1 4.3 %copy-start = (f32[64,16,1024]{2,1,0:T(8,128)S(1)}, f32[64,16,1024]{2,1,0:T(8,128)}, u32[]{:S(2)}) copy-start(f32[64,16,1024]{2,1,0:T(8,128)} %param.8) | copy-start | bytes 12582916
  125.9 47.8 %collective-permute-start.5 = (f32[32,16,1024]{2,1,0:T(8,128)S(1)}, f32[32,16,1024]{2,1,0:T(8,128)S(1)}, u32[]{:S(2)}, u32[]{:S(2)}) collective-permute-start(f32[32,16,1024]{2,1,0:T(8,128)S(1)} %slice.25), channel_id=1, source_target_pairs={{0,16},{8,24},{16,0},{24,8},{1,17},{9,25},{17,1},{25,9},{2,18},{10... | collective-permute-start | bytes 6291464 | tf_op jit(solution)/shard_map/ppermute | solution.py:176
  126.6 79.9 %collective-permute-start.3 = (f32[24,16,1024]{2,1,0:T(8,128)}, f32[24,16,1024]{2,1,0:T(8,128)}, u32[]{:S(2)}, u32[]{:S(2)}) collective-permute-start(f32[24,16,1024]{2,1,0:T(8,128)} %slice.24), channel_id=1, source_target_pairs={{0,16},{8,24},{16,0},{24,8},{1,17},{9,25},{17,1},{25,9},{2,18},{10... | collective-permute-start | bytes 4718600 | tf_op jit(solution)/shard_map/ppermute | solution.py:176
  173.6 36.7 %copy-start.1 = (f32[32,16,1024]{2,1,0:T(8,128)}, f32[32,16,1024]{2,1,0:T(8,128)S(1)}, u32[]{:S(2)}) copy-start(f32[32,16,1024]{2,1,0:T(8,128)S(1)} %collective-permute-done.5) | copy-start | bytes 6291460
  173.6 36.7 %collective-permute-start.6 = (f32[32,16,1024]{2,1,0:T(8,128)S(1)}, f32[32,16,1024]{2,1,0:T(8,128)}, u32[]{:S(2)}, u32[]{:S(2)}) collective-permute-start(f32[32,16,1024]{2,1,0:T(8,128)S(1)} %collective-permute-done.5), channel_id=1, source_target_pairs={{0,8},{8,0},{16,24},{24,16},{1,9},{9,1},{17,25},{25,17},{2,10},{10... | collective-permute-start | bytes 6291464 | tf_op jit(solution)/shard_map/ppermute | solution.py:178
  206.5 3.8 %collective-permute-start.4 = (f32[24,16,1024]{2,1,0:T(8,128)}, f32[24,16,1024]{2,1,0:T(8,128)}, u32[]{:S(2)}, u32[]{:S(2)}) collective-permute-start(f32[24,16,1024]{2,1,0:T(8,128)} %collective-permute-done.3), channel_id=1, source_target_pairs={{0,8},{8,0},{16,24},{24,16},{1,9},{9,1},{17,25},{25,17},{2,10},{10... | collective-permute-start | bytes 4718600 | tf_op jit(solution)/shard_map/ppermute | solution.py:178
  210.3 26.1 %copy-start.9 = (s32[256]{0:T(256)S(1)}, s32[256]{0:T(256)}, u32[]{:S(2)}) copy-start(s32[256]{0:T(256)} %param.15) | copy-start | bytes 3076
  224.2 17.1 %collective-permute-start.7 = (f32[64,1024]{1,0:T(8,128)}, f32[64,1024]{1,0:T(8,128)S(1)}, u32[]{:S(2)}, u32[]{:S(2)}) collective-permute-start(f32[64,1024]{1,0:T(8,128)} %get-tuple-element.16), channel_id=1, source_target_pairs={{0,1},{1,2},{2,3},{3,4},{4,5},{5,6},{6,7},{8,9},{9,10},{10,11},{11... | collective-permute-start | bytes 786440 | tf_op jit(solution)/shard_map/ppermute | solution.py:159
  226.1 15.2 %collective-permute-start.8 = (f32[64,1024]{1,0:T(8,128)}, f32[64,1024]{1,0:T(8,128)S(1)}, u32[]{:S(2)}, u32[]{:S(2)}) collective-permute-start(f32[64,1024]{1,0:T(8,128)} %get-tuple-element.17), channel_id=1, source_target_pairs={{1,0},{2,1},{3,2},{4,3},{5,4},{6,5},{7,6},{9,8},{10,9},{11,10},{12... | collective-permute-start | bytes 786440 | tf_op jit(solution)/shard_map/ppermute | solution.py:159
  231.2 10.1 %collective-permute-start.10 = (f32[1,1024]{1,0:T(1,128)S(1)}, f32[1,1024]{1,0:T(1,128)S(1)}, u32[]{:S(2)}, u32[]{:S(2)}) collective-permute-start(f32[1,1024]{1,0:T(1,128)S(1)} %get-tuple-element.23), channel_id=1, source_target_pairs={{1,0},{2,1},{3,2},{4,3},{5,4},{6,5},{7,6},{9,8},{10,9},{11,10},{12... | collective-permute-start | bytes 12296 | tf_op jit(solution)/shard_map/ppermute | solution.py:159
  233.1 8.2 %collective-permute-start.9 = (f32[1,1024]{1,0:T(1,128)S(1)}, f32[1,1024]{1,0:T(1,128)S(1)}, u32[]{:S(2)}, u32[]{:S(2)}) collective-permute-start(f32[1,1024]{1,0:T(1,128)S(1)} %get-tuple-element.24), channel_id=1, source_target_pairs={{0,1},{1,2},{2,3},{3,4},{4,5},{5,6},{6,7},{8,9},{9,10},{10,11},{11... | collective-permute-start | bytes 12296 | tf_op jit(solution)/shard_map/ppermute | solution.py:159
  241.2 0.6 copy-start.7
  241.2 0.6 copy-start.8
  241.2 0.7 copy-start.3
  241.3 0.8 copy-start.4
  266.3 8.6 %collective-permute-start.11 = (f32[64,1024]{1,0:T(8,128)}, f32[64,1024]{1,0:T(8,128)S(1)}, u32[]{:S(2)}, u32[]{:S(2)}) collective-permute-start(f32[64,1024]{1,0:T(8,128)} %get-tuple-element.19), channel_id=1, source_target_pairs={{0,1},{1,2},{2,3},{3,4},{4,5},{5,6},{6,7},{8,9},{9,10},{10,11},{11... | collective-permute-start | bytes 786440 | tf_op jit(solution)/shard_map/ppermute | solution.py:159
  268.2 12.4 %collective-permute-start.12 = (f32[64,1024]{1,0:T(8,128)}, f32[64,1024]{1,0:T(8,128)S(1)}, u32[]{:S(2)}, u32[]{:S(2)}) collective-permute-start(f32[64,1024]{1,0:T(8,128)} %get-tuple-element.20), channel_id=1, source_target_pairs={{1,0},{2,1},{3,2},{4,3},{5,4},{6,5},{7,6},{9,8},{10,9},{11,10},{12... | collective-permute-start | bytes 786440 | tf_op jit(solution)/shard_map/ppermute | solution.py:159
  274.8 5.7 %copy-start.5 = (f32[64,1024]{1,0:T(8,128)}, f32[64,1024]{1,0:T(8,128)S(1)}, u32[]{:S(2)}) copy-start(f32[64,1024]{1,0:T(8,128)S(1)} %collective-permute-done.11.above) | copy-start | bytes 786436
  280.6 0.7 copy-start.6
